TPU v7x, 32 devices: a whole 2x2x4 slice. The times are simulated.
32 devices in a mesh: rows: 2 (over y), cols: 4 (over z), slabs: 2 (over x), trial: 2 (over core).
Axes of the slice: x: 2, y: 2, z: 4, core: 2. Of those that a mesh axis runs over, the one named last changes fastest.
Arguments:
- field_values: float32 [64, 16, 256, 128], P(('trial', 'rows'), 'cols', 'slabs'), parts along dimension 0, may hold values from 0.5 to 2
- conductance: float32 [64, 16, 256, 128], P(('trial', 'rows'), 'cols', 'slabs'), parts along dimension 0, may hold values from 0.03 to 0.15
- source: float32 [64, 16, 256, 128], P(('trial', 'rows'), 'cols', 'slabs'), parts along dimension 0, may hold values from -0.2 to 0.2
Outputs:
- anomaly: float32 [64, 16, 256, 128], P(('trial', 'rows'), 'cols', 'slabs'), parts along dimension 0
- field_values_end: float32 [64, 16, 256, 128], P(('trial', 'rows'), 'cols', 'slabs'), parts along dimension 0
There are 2 independent parts, one for each index of `trial`. A program takes and returns all parts, laid end to end along the dimension named above; each array names one. Nothing has to cross between parts.
All inputs are finite; a program needn't handle non-finite values.
Results may differ from a plain program's by a relative error of at most 0.00002.
Values sent between devices are 32-bit elements; how exact they have to be, the bound alone decides.
A program may use at most 128 MiB of HBM per device.

v0:
```python
import functools

import jax
import jax.numpy as jnp
from jax import lax
from jax.experimental import pallas as pl
from jax.experimental.pallas import tpu as pltpu
from jax.sharding import PartitionSpec as P

STEPS = 4
TILE = 8
PIECES = 4
MESH = pl.DeviceIdType.MESH


def kernel(
    sizes, parts, field, conductance, source, scaled, last,
    u, cond, src, own, others,
    load_sem, send_sem, recv_sem, ksend_sem, krecv_sem, ssend_sem, srecv_sem,
):
    rows, cols, slabs = sizes
    nj, ni, nk, _ = field.shape
    row, col, slab = (lax.axis_index(name) for name in ("rows", "cols", "slabs"))
    has = {
        "i-": col > 0, "i+": col < cols - 1,
        "j-": row > 0, "j+": row < rows - 1,
        "k-": slab > 0, "k+": slab < slabs - 1,
    }
    to = {
        "i-": {"cols": jnp.maximum(col - 1, 0)}, "i+": {"cols": jnp.minimum(col + 1, cols - 1)},
        "j-": {"rows": jnp.maximum(row - 1, 0)}, "j+": {"rows": jnp.minimum(row + 1, rows - 1)},
        "k-": {"slabs": jnp.maximum(slab - 1, 0)}, "k+": {"slabs": jnp.minimum(slab + 1, slabs - 1)},
    }
    opposite = {"i-": "i+", "i+": "i-", "j-": "j+", "j+": "j-", "k-": "k+", "k+": "k-"}
    sides = ("i-", "i+", "j-", "j+")
    descending = lax.rem(slab, 2) == 0

    loads = [
        pltpu.make_async_copy(field, u.at[0, pl.ds(1, nj), pl.ds(1, ni), pl.ds(TILE, nk)], load_sem.at[0]),
        pltpu.make_async_copy(conductance, cond, load_sem.at[1]),
        pltpu.make_async_copy(source, src, load_sem.at[2]),
    ]
    loads[0].start()

    barrier = pltpu.get_barrier_semaphore()
    expected = rows - 1
    for off in range(1, rows):
        pl.semaphore_signal(barrier, inc=1, device_id={"rows": lax.rem(row + off, rows)}, device_id_type=MESH)
    for side in ("i-", "i+", "k-", "k+"):
        expected = expected + jnp.where(has[side], 1, 0)

        @pl.when(has[side])
        def _():
            pl.semaphore_signal(barrier, inc=1, device_id=to[side], device_id_type=MESH)

    pl.semaphore_wait(barrier, expected)

    def start_of(t, n):
        before, size = sum(parts[t][:n]), parts[t][n]
        return pl.multiple_of(jnp.where(descending, nk - before - size, before), TILE)

    def edges_of(t, n):
        first, final = n == 0, n == len(parts[t]) - 1
        low = jnp.where(descending, final, first)
        high = jnp.where(descending, first, final)
        return low, high

    def face(side, t, n, first):
        k0, kq = start_of(t, n), parts[t][n]
        inner = pl.ds(pl.multiple_of(TILE + k0, TILE), kq)
        js, is_ = pl.ds(1, nj), pl.ds(1, ni)
        if side[0] == "i":
            here, there = (1, ni + 1) if side == "i-" else (ni, 0)
            dst = u.at[t, js, there, inner]
            start = field.at[:, here - 1, pl.ds(k0, kq)] if first else u.at[t, js, here, inner]
        else:
            here, there = (1, nj + 1) if side == "j-" else (nj, 0)
            dst = u.at[t, there, is_, inner]
            start = field.at[here - 1, :, pl.ds(k0, kq)] if first else u.at[t, here, is_, inner]
        d = sides.index(side)
        return pltpu.make_async_remote_copy(
            src_ref=start, dst_ref=dst, send_sem=send_sem.at[d, t, n], recv_sem=recv_sem.at[d, t, n],
            device_id=to[side], device_id_type=MESH,
        )

    def kface(side, t, first):
        js, is_ = pl.ds(1, nj), pl.ds(1, ni)
        here, there = (TILE, TILE + nk) if side == "k-" else (nk, 0)
        start = field.at[:, :, pl.ds(here - TILE, TILE)] if first else u.at[t, js, is_, pl.ds(here, TILE)]
        d = 0 if side == "k-" else 1
        return pltpu.make_async_remote_copy(
            src_ref=start, dst_ref=u.at[t, js, is_, pl.ds(there, TILE)],
            send_sem=ksend_sem.at[d, t], recv_sem=krecv_sem.at[d, t],
            device_id=to[side], device_id_type=MESH,
        )

    def send_faces(t, n, first):
        low, high = edges_of(t, n)
        for side in sides:
            @pl.when(has[side])
            def _():
                face(side, t, n, first).start()

        @pl.when(low & has["k-"])
        def _():
            kface("k-", t, first).start()

        @pl.when(high & has["k+"])
        def _():
            kface("k+", t, first).start()

    def wait_faces(t, n):
        low, high = edges_of(t, n)
        for side in sides:
            @pl.when(has[opposite[side]])
            def _():
                face(side, t, n, False).wait_recv()

        @pl.when(high & has["k+"])
        def _():
            kface("k-", t, False).wait_recv()

        @pl.when(low & has["k-"])
        def _():
            kface("k+", t, False).wait_recv()

    for n in range(len(parts[0])):
        send_faces(0, n, True)

    loads[1].start()
    loads[2].start()

    def zero_plane(t, j, i):
        u[t, j, i, pl.ds(TILE, nk)] = jnp.zeros((nk, u.shape[-1]), u.dtype)

    @pl.loop(0, STEPS)
    def _(t):
        for side, i in (("i-", 0), ("i+", ni + 1)):
            @pl.when(jnp.logical_not(has[side]))
            def _():
                @pl.loop(0, nj)
                def _(j):
                    zero_plane(t, j + 1, i)

        for side, j in (("j-", 0), ("j+", nj + 1)):
            @pl.when(jnp.logical_not(has[side]))
            def _():
                for i in range(ni):
                    zero_plane(t, j, i + 1)

        for side, k in (("k-", 0), ("k+", TILE + nk)):
            @pl.when(jnp.logical_not(has[side]))
            def _():
                @pl.loop(0, nj)
                def _(j):
                    for i in range(ni):
                        u[t, j + 1, i + 1, pl.ds(k, TILE)] = jnp.zeros((TILE, u.shape[-1]), u.dtype)

    for load in loads:
        load.wait()

    def stencil(t, j, i, k0, kq):
        inner = pl.ds(pl.multiple_of(TILE + k0, TILE), kq)
        tall = u[t, j + 1, i + 1, pl.ds(k0, kq + 2 * TILE)]
        middle = tall[TILE:TILE + kq]
        spread = u[t, j, i + 1, inner] + u[t, j + 2, i + 1, inner]
        spread = spread + u[t, j + 1, i, inner] + u[t, j + 1, i + 2, inner]
        spread = spread + tall[TILE - 1:TILE - 1 + kq] + tall[TILE + 1:TILE + 1 + kq]
        spread = spread - 6.0 * middle
        own_k = pl.ds(k0, kq)
        return middle + cond[j, i, own_k] * spread + src[j, i, own_k]

    def middle_step(t, n):
        k0, kq = start_of(t, n), parts[t][n]
        wait_faces(t, n)

        @pl.loop(0, nj)
        def _(jj):
            j = lax.rem(jj + nj - 1, nj)
            for i in range(ni):
                u[t + 1, j + 1, i + 1, pl.ds(pl.multiple_of(TILE + k0, TILE), kq)] = stencil(t, j, i, k0, kq)

        low, done = sum(parts[t][:n]), sum(parts[t][:n + 1])
        for m in range(len(parts[t + 1])):
            if low <= sum(parts[t + 1][:m]) < done:
                send_faces(t + 1, m, False)

    for t in range(STEPS - 1):
        for n in range(len(parts[t])):
            middle_step(t, n)

    final = parts[STEPS - 1]

    def span_of(n):
        return pl.ds(start_of(STEPS - 1, n), final[n])

    def stats_copy(off, n):
        return pltpu.make_async_remote_copy(
            src_ref=own.at[:, :, span_of(n)], dst_ref=others.at[off - 1, :, :, span_of(n)],
            send_sem=ssend_sem.at[off - 1, n], recv_sem=srecv_sem.at[off - 1, n],
            device_id={"rows": lax.rem(row + off, rows)}, device_id_type=MESH,
        )

    def final_step(n):
        k0, kq, ks = start_of(STEPS - 1, n), final[n], span_of(n)
        wait_faces(STEPS - 1, n)
        zero = jnp.zeros((kq, u.shape[-1]), u.dtype)
        for i in range(ni):
            def step(j, total):
                new = stencil(STEPS - 1, j, i, k0, kq)
                last[j, i, ks] = new
                return total + new

            mean = lax.fori_loop(0, nj, step, zero, unroll=2) / nj
            own[0, i, ks] = mean

            def spread_of(j, total):
                away = last[j, i, ks] - mean
                return total + away * away

            own[1, i, ks] = lax.fori_loop(0, nj, spread_of, zero, unroll=2)
        for off in range(1, rows):
            stats_copy(off, n).start()

    def finish(n):
        ks = span_of(n)
        for off in range(1, rows):
            stats_copy(off, n).wait_recv()
        for i in range(ni):
            means = [own[0, i, ks]] + [others[off - 1, 0, i, ks] for off in range(1, rows)]
            spreads = [own[1, i, ks]] + [others[off - 1, 1, i, ks] for off in range(1, rows)]
            mean = sum(means[1:], means[0]) / rows
            spread = sum(spreads[1:], spreads[0])
            for other in means:
                spread = spread + nj * ((other - mean) * (other - mean))
            scale = lax.rsqrt(spread / (nj * rows) + 0.0001)

            @pl.loop(0, nj)
            def _(j):
                scaled[j, i, ks] = (last[j, i, ks] - mean) * scale

    for n in range(len(final)):
        final_step(n)
        if n > 0:
            finish(n - 1)
    finish(len(final) - 1)

    for t in range(STEPS):
        for side in sides:
            @pl.when(has[side])
            def _():
                for n in range(len(parts[t])):
                    face(side, t, n, False).wait_send()

        for side in ("k-", "k+"):
            @pl.when(has[side])
            def _():
                kface(side, t, False).wait_send()

    for n in range(len(final)):
        for off in range(1, rows):
            stats_copy(off, n).wait_send()


def write_out(near_anomaly, near_field, anomaly, field_end, sems):
    copies = []
    for which, (start, dst) in enumerate(((near_field, field_end), (near_anomaly, anomaly))):
        pieces = sems.shape[1]
        depth = start.shape[0] // pieces
        for piece in range(pieces):
            js = pl.ds(piece * depth, depth)
            copies.append(pltpu.make_async_copy(start.at[js], dst.at[js], sems.at[which, piece]))
    for copy in copies:
        copy.start()
    for copy in copies:
        copy.wait()


def parts_of(nk):
    half = nk // 2 if nk % (2 * TILE) == 0 else nk
    coarse = (half,) * (nk // half)
    small = half * 3 // 8 // TILE * TILE
    fine = coarse[:-1] + ((half - small, small) if small else (half,))
    return (coarse,) * (STEPS - 1) + (fine,)


def on_device(field_values, conductance, source):
    sizes = tuple(lax.axis_size(name) for name in ("rows", "cols", "slabs"))
    nj, ni, nk, levels = field_values.shape
    parts = parts_of(nk)
    most = max(len(of) for of in parts)
    peers = max(sizes[0] - 1, 1)
    whole = pltpu.VMEM(field_values.shape, field_values.dtype)
    near = pl.BlockSpec(memory_space=pltpu.VMEM)
    anywhere = pl.BlockSpec(memory_space=pl.ANY)
    results = pl.pallas_call(
        functools.partial(kernel, sizes, parts),
        out_shape=(whole, whole),
        in_specs=[anywhere] * 3,
        out_specs=(near, near),
        scratch_shapes=[
            pltpu.VMEM((STEPS, nj + 2, ni + 2, nk + 2 * TILE, levels), jnp.float32),
            pltpu.VMEM((nj, ni, nk, levels), jnp.float32),
            pltpu.VMEM((nj, ni, nk, levels), jnp.float32),
            pltpu.VMEM((2, ni, nk, levels), jnp.float32),
            pltpu.VMEM((peers, 2, ni, nk, levels), jnp.float32),
            pltpu.SemaphoreType.DMA((3,)),
            pltpu.SemaphoreType.DMA((4, STEPS, most)),
            pltpu.SemaphoreType.DMA((4, STEPS, most)),
            pltpu.SemaphoreType.DMA((2, STEPS)),
            pltpu.SemaphoreType.DMA((2, STEPS)),
            pltpu.SemaphoreType.DMA((peers, most)),
            pltpu.SemaphoreType.DMA((peers, most)),
        ],
        compiler_params=pltpu.CompilerParams(
            collective_id=0, has_side_effects=True, vmem_limit_bytes=52 * 1024 * 1024
        ),
        name="heat_steps",
    )(field_values, conductance, source)
    there = jax.ShapeDtypeStruct(field_values.shape, field_values.dtype)
    pieces = PIECES if nj % PIECES == 0 else 1
    return pl.pallas_call(
        write_out,
        out_shape=(there, there),
        in_specs=[near] * 2,
        out_specs=(anywhere, anywhere),
        scratch_shapes=[pltpu.SemaphoreType.DMA((2, pieces))],
        compiler_params=pltpu.CompilerParams(vmem_limit_bytes=1024 * 1024),
        name="write_out",
    )(*results)


def solution(mesh):
    spec = P(("trial", "rows"), "cols", "slabs", None)
    return jax.shard_map(
        on_device, mesh=mesh, in_specs=(spec,) * 3, out_specs=(spec, spec), check_vma=False
    )
```

profile of v0, /device:TPU:0, one launch (start us, length us, event | category | flops | bytes accessed | tf_op | source)
XLA Modules:
  0.0 106.0 jit_solution(3824230407495583549)
XLA Ops:
  0.6 102.0 %heat_steps.1 = (f32[16,4,128,128]{3,2,1,0:T(8,128)S(1)}, f32[16,4,128,128]{3,2,1,0:T(8,128)S(1)}) custom-call(f32[16,4,128,128]{3,2,1,0:T(8,128)} %field.1, f32[16,4,128,128]{3,2,1,0:T(8,128)} %conductance.1, f32[16,4,128,128]{3,2,1,0:T(8,128)} %source.1), custom_call_target="tpu_custom_call" | custom-call | tf_op jit(solution)/shard_map/heat_steps/pallas_call | solution.py:296
  102.6 3.4 %write_out.1 = (f32[16,4,128,128]{3,2,1,0:T(8,128)}, f32[16,4,128,128]{3,2,1,0:T(8,128)}) custom-call(f32[16,4,128,128]{3,2,1,0:T(8,128)S(1)} %get-tuple-element.4.near_anomaly, f32[16,4,128,128]{3,2,1,0:T(8,128)S(1)} %get-tuple-element.5.near_field), custom_call_target="tpu_custom_call" | custom-call | tf_op jit(solution)/shard_map/write_out/pallas_call | solution.py:322
where the time goes:
time: 106 us
  Pallas kernels  105 us (99%)
    pallas_call x1, Pallas kernels, on_device(): pl.pallas_call(functools.partial(kernel, sizes, parts), out_shape=(whole,...  102 us
    pallas_call x1, Pallas kernels, on_device(): pl.pallas_call(write_out, out_shape=(there, there), in_specs=[near] * 2,...  3.37 us

commit v1 on v0

--- a/solution.py
+++ b/solution.py
@@ -10,13 +10,15 @@
 STEPS = 4
 TILE = 8
 PIECES = 4
+FINE = (5, 2)
+SHORT = 128
 MESH = pl.DeviceIdType.MESH
 
 
 def kernel(
-    sizes, parts, field, conductance, source, scaled, last,
+    sizes, coarse, parts, field, conductance, source, scaled, last,
     u, cond, src, own, others,
-    load_sem, send_sem, recv_sem, ksend_sem, krecv_sem, ssend_sem, srecv_sem,
+    load_sem, send_sem, recv_sem, jsend_sem, jrecv_sem, ksend_sem, krecv_sem, ssend_sem, srecv_sem,
 ):
     rows, cols, slabs = sizes
     nj, ni, nk, _ = field.shape
@@ -32,7 +34,6 @@
         "k-": {"slabs": jnp.maximum(slab - 1, 0)}, "k+": {"slabs": jnp.minimum(slab + 1, slabs - 1)},
     }
     opposite = {"i-": "i+", "i+": "i-", "j-": "j+", "j+": "j-", "k-": "k+", "k+": "k-"}
-    sides = ("i-", "i+", "j-", "j+")
     descending = lax.rem(slab, 2) == 0
 
     loads = [
@@ -55,18 +56,19 @@
 
     pl.semaphore_wait(barrier, expected)
 
-    def start_of(t, n):
-        before, size = sum(parts[t][:n]), parts[t][n]
+    def start_of(of, n):
+        before, size = sum(of[:n]), of[n]
         return pl.multiple_of(jnp.where(descending, nk - before - size, before), TILE)
 
-    def edges_of(t, n):
-        first, final = n == 0, n == len(parts[t]) - 1
+    def edges_of(n):
+        first, final = n == 0, n == len(coarse) - 1
         low = jnp.where(descending, final, first)
         high = jnp.where(descending, first, final)
         return low, high
 
     def face(side, t, n, first):
-        k0, kq = start_of(t, n), parts[t][n]
+        of = parts[t] if side[0] == "i" else coarse
+        k0, kq = start_of(of, n), of[n]
         inner = pl.ds(pl.multiple_of(TILE + k0, TILE), kq)
         js, is_ = pl.ds(1, nj), pl.ds(1, ni)
         if side[0] == "i":
@@ -77,9 +79,10 @@
             here, there = (1, nj + 1) if side == "j-" else (nj, 0)
             dst = u.at[t, there, is_, inner]
             start = field.at[here - 1, :, pl.ds(k0, kq)] if first else u.at[t, here, is_, inner]
-        d = sides.index(side)
+        d = 0 if side[1] == "-" else 1
+        sent, received = (send_sem, recv_sem) if side[0] == "i" else (jsend_sem, jrecv_sem)
         return pltpu.make_async_remote_copy(
-            src_ref=start, dst_ref=dst, send_sem=send_sem.at[d, t, n], recv_sem=recv_sem.at[d, t, n],
+            src_ref=start, dst_ref=dst, send_sem=sent.at[d, t, n], recv_sem=received.at[d, t, n],
             device_id=to[side], device_id_type=MESH,
         )
 
@@ -94,12 +97,23 @@
             device_id=to[side], device_id_type=MESH,
         )
 
+    def fine_of(t, n):
+        low, done = sum(coarse[:n]), sum(coarse[:n + 1])
+        return [m for m in range(len(parts[t])) if low <= sum(parts[t][:m]) < done]
+
     def send_faces(t, n, first):
-        low, high = edges_of(t, n)
-        for side in sides:
+        for side in ("i-", "i+"):
             @pl.when(has[side])
             def _():
+                for m in fine_of(t, n):
+                    face(side, t, m, first).start()
+
+        for side in ("j-", "j+"):
+            @pl.when(has[side])
+            def _():
                 face(side, t, n, first).start()
+
+        low, high = edges_of(n)
 
         @pl.when(low & has["k-"])
         def _():
@@ -109,12 +123,19 @@
         def _():
             kface("k+", t, first).start()
 
-    def wait_faces(t, n):
-        low, high = edges_of(t, n)
-        for side in sides:
+    def wait_i(t, n):
+        for side in ("i-", "i+"):
             @pl.when(has[opposite[side]])
             def _():
                 face(side, t, n, False).wait_recv()
+
+    def wait_others(t, n):
+        for side in ("j-", "j+"):
+            @pl.when(has[opposite[side]])
+            def _():
+                face(side, t, n, False).wait_recv()
+
+        low, high = edges_of(n)
 
         @pl.when(high & has["k+"])
         def _():
@@ -124,7 +145,25 @@
         def _():
             kface("k+", t, False).wait_recv()
 
-    for n in range(len(parts[0])):
+    def wait_sent(t):
+        for side in ("i-", "i+"):
+            @pl.when(has[side])
+            def _():
+                for n in range(len(parts[t])):
+                    face(side, t, n, False).wait_send()
+
+        for side in ("j-", "j+"):
+            @pl.when(has[side])
+            def _():
+                for n in range(len(coarse)):
+                    face(side, t, n, False).wait_send()
+
+        for side in ("k-", "k+"):
+            @pl.when(has[side])
+            def _():
+                kface(side, t, False).wait_send()
+
+    for n in range(len(coarse)):
         send_faces(0, n, True)
 
     loads[1].start()
@@ -171,8 +210,10 @@
         return middle + cond[j, i, own_k] * spread + src[j, i, own_k]
 
     def middle_step(t, n):
-        k0, kq = start_of(t, n), parts[t][n]
-        wait_faces(t, n)
+        k0, kq = start_of(coarse, n), coarse[n]
+        for m in fine_of(t, n):
+            wait_i(t, m)
+        wait_others(t, n)
 
         @pl.loop(0, nj)
         def _(jj):
@@ -180,86 +221,103 @@
             for i in range(ni):
                 u[t + 1, j + 1, i + 1, pl.ds(pl.multiple_of(TILE + k0, TILE), kq)] = stencil(t, j, i, k0, kq)
 
-        low, done = sum(parts[t][:n]), sum(parts[t][:n + 1])
-        for m in range(len(parts[t + 1])):
-            if low <= sum(parts[t + 1][:m]) < done:
-                send_faces(t + 1, m, False)
+        send_faces(t + 1, n, False)
 
     for t in range(STEPS - 1):
-        for n in range(len(parts[t])):
+        for n in range(len(coarse)):
             middle_step(t, n)
-
-    final = parts[STEPS - 1]
-
-    def span_of(n):
-        return pl.ds(start_of(STEPS - 1, n), final[n])
-
-    def stats_copy(off, n):
+        if t > 0:
+            wait_sent(t - 1)
+
+    t = STEPS - 1
+    final = parts[t]
+    outer = tuple(range(ni)) if ni < 3 else (0, ni - 1)
+    inner = tuple(range(1, ni - 1)) if ni > 2 else ()
+    groups = [(outer, 0, final, n, n) for n in range(len(final))]
+    if inner:
+        groups = [(inner, len(outer), coarse, n, len(final) + n) for n in range(len(coarse))] + groups
+
+    def stats_copy(off, group):
+        planes, at, of, n, sem = group
+        place = (slice(None), pl.ds(at, len(planes)), pl.ds(start_of(of, n), of[n]))
         return pltpu.make_async_remote_copy(
-            src_ref=own.at[:, :, span_of(n)], dst_ref=others.at[off - 1, :, :, span_of(n)],
-            send_sem=ssend_sem.at[off - 1, n], recv_sem=srecv_sem.at[off - 1, n],
+            src_ref=own.at[place], dst_ref=others.at[(off - 1,) + place],
+            send_sem=ssend_sem.at[off - 1, sem], recv_sem=srecv_sem.at[off - 1, sem],
             device_id={"rows": lax.rem(row + off, rows)}, device_id_type=MESH,
         )
 
-    def final_step(n):
-        k0, kq, ks = start_of(STEPS - 1, n), final[n], span_of(n)
-        wait_faces(STEPS - 1, n)
+    def final_step(group):
+        planes, at, of, n, _ = group
+        k0, kq = start_of(of, n), of[n]
+        ks = pl.ds(k0, kq)
         zero = jnp.zeros((kq, u.shape[-1]), u.dtype)
-        for i in range(ni):
+        for p, i in enumerate(planes):
+            if kq * nj <= SHORT:
+                news = [stencil(t, j, i, k0, kq) for j in range(nj)]
+                mean = sum(news[1:], news[0]) / nj
+                own[0, at + p, ks] = mean
+                aways = [new - mean for new in news]
+                squares = [away * away for away in aways]
+                own[1, at + p, ks] = sum(squares[1:], squares[0])
+                for j in range(nj):
+                    last[j, i, ks] = news[j]
+                continue
+
             def step(j, total):
-                new = stencil(STEPS - 1, j, i, k0, kq)
+                new = stencil(t, j, i, k0, kq)
                 last[j, i, ks] = new
                 return total + new
 
             mean = lax.fori_loop(0, nj, step, zero, unroll=2) / nj
-            own[0, i, ks] = mean
+            own[0, at + p, ks] = mean
 
             def spread_of(j, total):
                 away = last[j, i, ks] - mean
                 return total + away * away
 
-            own[1, i, ks] = lax.fori_loop(0, nj, spread_of, zero, unroll=2)
+            own[1, at + p, ks] = lax.fori_loop(0, nj, spread_of, zero, unroll=2)
         for off in range(1, rows):
-            stats_copy(off, n).start()
-
-    def finish(n):
-        ks = span_of(n)
+            stats_copy(off, group).start()
+
+    def finish(group):
+        planes, at, of, n, _ = group
+        kq = of[n]
+        ks = pl.ds(start_of(of, n), kq)
         for off in range(1, rows):
-            stats_copy(off, n).wait_recv()
-        for i in range(ni):
-            means = [own[0, i, ks]] + [others[off - 1, 0, i, ks] for off in range(1, rows)]
-            spreads = [own[1, i, ks]] + [others[off - 1, 1, i, ks] for off in range(1, rows)]
+            stats_copy(off, group).wait_recv()
+        for p, i in enumerate(planes):
+            means = [own[0, at + p, ks]] + [others[off - 1, 0, at + p, ks] for off in range(1, rows)]
+            spreads = [own[1, at + p, ks]] + [others[off - 1, 1, at + p, ks] for off in range(1, rows)]
             mean = sum(means[1:], means[0]) / rows
             spread = sum(spreads[1:], spreads[0])
             for other in means:
                 spread = spread + nj * ((other - mean) * (other - mean))
             scale = lax.rsqrt(spread / (nj * rows) + 0.0001)
+            if kq * nj <= SHORT:
+                for j in range(nj):
+                    scaled[j, i, ks] = (last[j, i, ks] - mean) * scale
+                continue
 
             @pl.loop(0, nj)
             def _(j):
                 scaled[j, i, ks] = (last[j, i, ks] - mean) * scale
 
-    for n in range(len(final)):
-        final_step(n)
-        if n > 0:
-            finish(n - 1)
-    finish(len(final) - 1)
-
-    for t in range(STEPS):
-        for side in sides:
-            @pl.when(has[side])
-            def _():
-                for n in range(len(parts[t])):
-                    face(side, t, n, False).wait_send()
-
-        for side in ("k-", "k+"):
-            @pl.when(has[side])
-            def _():
-                kface(side, t, False).wait_send()
-
-    for n in range(len(final)):
+    for n in range(len(coarse)):
+        wait_others(t, n)
+    for at, group in enumerate(groups):
+        if group[0] is outer:
+            wait_i(t, group[3])
+        final_step(group)
+        if at > 0:
+            finish(groups[at - 1])
+        if at == len(groups) - 2:
+            wait_sent(STEPS - 2)
+    finish(groups[-1])
+
+    wait_sent(t)
+    for group in groups:
         for off in range(1, rows):
-            stats_copy(off, n).wait_send()
+            stats_copy(off, group).wait_send()
 
 
 def write_out(near_anomaly, near_field, anomaly, field_end, sems):
@@ -279,22 +337,27 @@
 def parts_of(nk):
     half = nk // 2 if nk % (2 * TILE) == 0 else nk
     coarse = (half,) * (nk // half)
-    small = half * 3 // 8 // TILE * TILE
-    fine = coarse[:-1] + ((half - small, small) if small else (half,))
-    return (coarse,) * (STEPS - 1) + (fine,)
+    fine, left = [], half
+    for eighths in FINE:
+        size = half * eighths // 8 // TILE * TILE
+        if 0 < size < left:
+            fine.append(size)
+            left -= size
+    return coarse, (coarse,) * (STEPS - 1) + (coarse[:-1] + tuple(fine) + (left,),)
 
 
 def on_device(field_values, conductance, source):
     sizes = tuple(lax.axis_size(name) for name in ("rows", "cols", "slabs"))
     nj, ni, nk, levels = field_values.shape
-    parts = parts_of(nk)
+    coarse, parts = parts_of(nk)
     most = max(len(of) for of in parts)
+    groups = len(parts[-1]) + len(coarse)
     peers = max(sizes[0] - 1, 1)
     whole = pltpu.VMEM(field_values.shape, field_values.dtype)
     near = pl.BlockSpec(memory_space=pltpu.VMEM)
     anywhere = pl.BlockSpec(memory_space=pl.ANY)
     results = pl.pallas_call(
-        functools.partial(kernel, sizes, parts),
+        functools.partial(kernel, sizes, coarse, parts),
         out_shape=(whole, whole),
         in_specs=[anywhere] * 3,
         out_specs=(near, near),
@@ -305,12 +368,14 @@
             pltpu.VMEM((2, ni, nk, levels), jnp.float32),
             pltpu.VMEM((peers, 2, ni, nk, levels), jnp.float32),
             pltpu.SemaphoreType.DMA((3,)),
-            pltpu.SemaphoreType.DMA((4, STEPS, most)),
-            pltpu.SemaphoreType.DMA((4, STEPS, most)),
+            pltpu.SemaphoreType.DMA((2, STEPS, most)),
+            pltpu.SemaphoreType.DMA((2, STEPS, most)),
+            pltpu.SemaphoreType.DMA((2, STEPS, len(coarse))),
+            pltpu.SemaphoreType.DMA((2, STEPS, len(coarse))),
             pltpu.SemaphoreType.DMA((2, STEPS)),
             pltpu.SemaphoreType.DMA((2, STEPS)),
-            pltpu.SemaphoreType.DMA((peers, most)),
-            pltpu.SemaphoreType.DMA((peers, most)),
+            pltpu.SemaphoreType.DMA((peers, groups)),
+            pltpu.SemaphoreType.DMA((peers, groups)),
         ],
         compiler_params=pltpu.CompilerParams(
             collective_id=0, has_side_effects=True, vmem_limit_bytes=52 * 1024 * 1024

time: 106 us -> 105 us (level)
    pallas_call x1, Pallas kernels: 102 us -> 101 us  [on_device(): pl.pallas_call(functools.partial(kernel, sizes, coarse, parts), out_shape...]
where the time goes in v1:
time: 105 us
  Pallas kernels  104 us (99%)
    pallas_call x1, Pallas kernels, on_device(): pl.pallas_call(functools.partial(kernel, sizes, coarse, parts), out_shape...  101 us
    pallas_call x1, Pallas kernels, on_device(): pl.pallas_call(write_out, out_shape=(there, there), in_specs=[near] * 2,...  3.37 us

profile of v1, /device:TPU:0, one launch (start us, length us, event | category | flops | bytes accessed | tf_op | source)
XLA Modules:
  0.0 104.7 jit_solution(3665948155317643665)
XLA Ops:
  0.6 100.7 %heat_steps.1 = (f32[16,4,128,128]{3,2,1,0:T(8,128)S(1)}, f32[16,4,128,128]{3,2,1,0:T(8,128)S(1)}) custom-call(f32[16,4,128,128]{3,2,1,0:T(8,128)} %field.1, f32[16,4,128,128]{3,2,1,0:T(8,128)} %conductance.1, f32[16,4,128,128]{3,2,1,0:T(8,128)} %source.1), custom_call_target="tpu_custom_call" | custom-call | tf_op jit(solution)/shard_map/heat_steps/pallas_call | solution.py:359
  101.3 3.4 %write_out.1 = (f32[16,4,128,128]{3,2,1,0:T(8,128)}, f32[16,4,128,128]{3,2,1,0:T(8,128)}) custom-call(f32[16,4,128,128]{3,2,1,0:T(8,128)S(1)} %get-tuple-element.4.near_anomaly, f32[16,4,128,128]{3,2,1,0:T(8,128)S(1)} %get-tuple-element.5.near_field), custom_call_target="tpu_custom_call" | custom-call | tf_op jit(solution)/shard_map/write_out/pallas_call | solution.py:387

commit v2 on v1

--- a/solution.py
+++ b/solution.py
@@ -12,6 +12,8 @@
 PIECES = 4
 FINE = (5, 2)
 SHORT = 128
+YIELD = 1
+PAUSE = 2000
 MESH = pl.DeviceIdType.MESH
 
 
@@ -34,6 +36,7 @@
         "k-": {"slabs": jnp.maximum(slab - 1, 0)}, "k+": {"slabs": jnp.minimum(slab + 1, slabs - 1)},
     }
     opposite = {"i-": "i+", "i+": "i-", "j-": "j+", "j+": "j-", "k-": "k+", "k+": "k-"}
+    first_core = lax.rem(lax.axis_index("trial"), 2) == 0
     descending = lax.rem(slab, 2) == 0
 
     loads = [
@@ -145,13 +148,15 @@
         def _():
             kface("k+", t, False).wait_recv()
 
-    def wait_sent(t):
+    def wait_sent_i(t, who):
         for side in ("i-", "i+"):
-            @pl.when(has[side])
+            @pl.when(who & has[side])
             def _():
                 for n in range(len(parts[t])):
                     face(side, t, n, False).wait_send()
 
+    def wait_sent(t):
+        wait_sent_i(t, first_core if t == YIELD else True)
         for side in ("j-", "j+"):
             @pl.when(has[side])
             def _():
@@ -220,6 +225,13 @@
             j = lax.rem(jj + nj - 1, nj)
             for i in range(ni):
                 u[t + 1, j + 1, i + 1, pl.ds(pl.multiple_of(TILE + k0, TILE), kq)] = stencil(t, j, i, k0, kq)
+
+        if t == YIELD and n == 0:
+            wait_sent_i(t, jnp.logical_not(first_core))
+
+            @pl.when(jnp.logical_not(first_core))
+            def _():
+                pl.delay(PAUSE)
 
         send_faces(t + 1, n, False)
 

time: 105 us -> 103 us (0.981)
  Pallas kernels: 104 us -> 102 us
    pallas_call x1, Pallas kernels: 101 us -> 98.4 us  [on_device(): pl.pallas_call(functools.partial(kernel, sizes, coarse, parts), out_shape...]
where the time goes in v2:
time: 103 us; the launch traced here: 102 us
  Pallas kernels  102 us (99%)
    pallas_call x1, Pallas kernels, on_device(): pl.pallas_call(functools.partial(kernel, sizes, coarse, parts), out_shape...  98.4 us
    pallas_call x1, Pallas kernels, on_device(): pl.pallas_call(write_out, out_shape=(there, there), in_specs=[near] * 2,...  3.37 us

profile of v2, /device:TPU:0, one launch (start us, length us, event | category | flops | bytes accessed | tf_op | source)
XLA Modules:
  0.0 102.4 jit_solution(16795723246878864729)
XLA Ops:
  0.6 98.4 %heat_steps.1 = (f32[16,4,128,128]{3,2,1,0:T(8,128)S(1)}, f32[16,4,128,128]{3,2,1,0:T(8,128)S(1)}) custom-call(f32[16,4,128,128]{3,2,1,0:T(8,128)} %field.1, f32[16,4,128,128]{3,2,1,0:T(8,128)} %conductance.1, f32[16,4,128,128]{3,2,1,0:T(8,128)} %source.1), custom_call_target="tpu_custom_call" | custom-call | tf_op jit(solution)/shard_map/heat_steps/pallas_call | solution.py:371
  99.0 3.4 %write_out.1 = (f32[16,4,128,128]{3,2,1,0:T(8,128)}, f32[16,4,128,128]{3,2,1,0:T(8,128)}) custom-call(f32[16,4,128,128]{3,2,1,0:T(8,128)S(1)} %get-tuple-element.4.near_anomaly, f32[16,4,128,128]{3,2,1,0:T(8,128)S(1)} %get-tuple-element.5.near_field), custom_call_target="tpu_custom_call" | custom-call | tf_op jit(solution)/shard_map/write_out/pallas_call | solution.py:399

commit v3 on v2

--- a/solution.py
+++ b/solution.py
@@ -10,15 +10,14 @@
 STEPS = 4
 TILE = 8
 PIECES = 4
-FINE = (5, 2)
-SHORT = 128
+FINE = (4,)
 YIELD = 1
 PAUSE = 2000
 MESH = pl.DeviceIdType.MESH
 
 
 def kernel(
-    sizes, coarse, parts, field, conductance, source, scaled, last,
+    sizes, coarse, parts, field, conductance, source, scaled, last, late,
     u, cond, src, own, others,
     load_sem, send_sem, recv_sem, jsend_sem, jrecv_sem, ksend_sem, krecv_sem, ssend_sem, srecv_sem,
 ):
@@ -203,12 +202,14 @@
     for load in loads:
         load.wait()
 
-    def stencil(t, j, i, k0, kq):
+    def stencil(t, j, i, k0, kq, skip=(False, False)):
         inner = pl.ds(pl.multiple_of(TILE + k0, TILE), kq)
         tall = u[t, j + 1, i + 1, pl.ds(k0, kq + 2 * TILE)]
         middle = tall[TILE:TILE + kq]
         spread = u[t, j, i + 1, inner] + u[t, j + 2, i + 1, inner]
-        spread = spread + u[t, j + 1, i, inner] + u[t, j + 1, i + 2, inner]
+        for beside, left_out in ((i, skip[0]), (i + 2, skip[1])):
+            if not left_out:
+                spread = spread + u[t, j + 1, beside, inner]
         spread = spread + tall[TILE - 1:TILE - 1 + kq] + tall[TILE + 1:TILE + 1 + kq]
         spread = spread - 6.0 * middle
         own_k = pl.ds(k0, kq)
@@ -243,11 +244,9 @@
 
     t = STEPS - 1
     final = parts[t]
-    outer = tuple(range(ni)) if ni < 3 else (0, ni - 1)
-    inner = tuple(range(1, ni - 1)) if ni > 2 else ()
-    groups = [(outer, 0, final, n, n) for n in range(len(final))]
-    if inner:
-        groups = [(inner, len(outer), coarse, n, len(final) + n) for n in range(len(coarse))] + groups
+    outer, inner = planes_of(ni)
+    groups = [(inner, len(outer), coarse, n, n) for n in range(len(coarse))] if inner else []
+    groups += [(outer, 0, final, n, len(coarse) + n) for n in range(len(final) - 1)]
 
     def stats_copy(off, group):
         planes, at, of, n, sem = group
@@ -258,78 +257,114 @@
             device_id={"rows": lax.rem(row + off, rows)}, device_id_type=MESH,
         )
 
-    def final_step(group):
+    def blocks(of, n):
+        def wrap(body):
+            k0 = start_of(of, n)
+
+            @pl.loop(0, of[n] // TILE)
+            def _(b):
+                body(pl.multiple_of(k0 + b * TILE, TILE), pl.multiple_of(b * TILE, TILE))
+        return wrap
+
+    def sums_of(news):
+        mean = sum(news[1:], news[0]) / nj
+        aways = [new - mean for new in news]
+        squares = [away * away for away in aways]
+        return mean, sum(squares[1:], squares[0])
+
+    def inner_step(group):
         planes, at, of, n, _ = group
-        k0, kq = start_of(of, n), of[n]
-        ks = pl.ds(k0, kq)
-        zero = jnp.zeros((kq, u.shape[-1]), u.dtype)
-        for p, i in enumerate(planes):
-            if kq * nj <= SHORT:
-                news = [stencil(t, j, i, k0, kq) for j in range(nj)]
-                mean = sum(news[1:], news[0]) / nj
-                own[0, at + p, ks] = mean
-                aways = [new - mean for new in news]
-                squares = [away * away for away in aways]
-                own[1, at + p, ks] = sum(squares[1:], squares[0])
+
+        @blocks(of, n)
+        def _(k, b):
+            ks = pl.ds(k, TILE)
+            for p, i in enumerate(planes):
+                news = [stencil(t, j, i, k, TILE) for j in range(nj)]
+                own[0, at + p, ks], own[1, at + p, ks] = sums_of(news)
                 for j in range(nj):
                     last[j, i, ks] = news[j]
-                continue
-
-            def step(j, total):
-                new = stencil(t, j, i, k0, kq)
-                last[j, i, ks] = new
-                return total + new
-
-            mean = lax.fori_loop(0, nj, step, zero, unroll=2) / nj
-            own[0, at + p, ks] = mean
-
-            def spread_of(j, total):
-                away = last[j, i, ks] - mean
-                return total + away * away
-
-            own[1, at + p, ks] = lax.fori_loop(0, nj, spread_of, zero, unroll=2)
+
         for off in range(1, rows):
             stats_copy(off, group).start()
 
+    def outer_ahead(n):
+        @blocks(coarse, n)
+        def _(k, b):
+            for i in outer:
+                for j in range(nj):
+                    last[j, i, pl.ds(k, TILE)] = stencil(t, j, i, k, TILE, skip=(i == 0, i == ni - 1))
+
+    def outer_step(n, into):
+        @blocks(final, n)
+        def _(k, b):
+            ks, inside = pl.ds(k, TILE), pl.ds(pl.multiple_of(TILE + k, TILE), TILE)
+            for p, i in enumerate(outer):
+                faces = [face for face, here in ((0, i == 0), (ni + 1, i == ni - 1)) if here]
+                news = []
+                for j in range(nj):
+                    arrived = [u[t, j + 1, face, inside] for face in faces]
+                    news.append(last[j, i, ks] + cond[j, i, ks] * sum(arrived[1:], arrived[0]))
+                if into is own:
+                    own[0, p, ks], own[1, p, ks] = sums_of(news)
+                else:
+                    into[0, p, pl.ds(b, TILE)], into[1, p, pl.ds(b, TILE)] = sums_of(news)
+                for j in range(nj):
+                    last[j, i, ks] = news[j]
+
     def finish(group):
         planes, at, of, n, _ = group
-        kq = of[n]
-        ks = pl.ds(start_of(of, n), kq)
         for off in range(1, rows):
             stats_copy(off, group).wait_recv()
-        for p, i in enumerate(planes):
-            means = [own[0, at + p, ks]] + [others[off - 1, 0, at + p, ks] for off in range(1, rows)]
-            spreads = [own[1, at + p, ks]] + [others[off - 1, 1, at + p, ks] for off in range(1, rows)]
-            mean = sum(means[1:], means[0]) / rows
-            spread = sum(spreads[1:], spreads[0])
-            for other in means:
-                spread = spread + nj * ((other - mean) * (other - mean))
-            scale = lax.rsqrt(spread / (nj * rows) + 0.0001)
-            if kq * nj <= SHORT:
+
+        @blocks(of, n)
+        def _(k, b):
+            ks = pl.ds(k, TILE)
+            for p, i in enumerate(planes):
+                means = [own[0, at + p, ks]] + [others[off - 1, 0, at + p, ks] for off in range(1, rows)]
+                spreads = [own[1, at + p, ks]] + [others[off - 1, 1, at + p, ks] for off in range(1, rows)]
+                mean, scale = joined(nj, means, spreads)
                 for j in range(nj):
                     scaled[j, i, ks] = (last[j, i, ks] - mean) * scale
-                continue
-
-            @pl.loop(0, nj)
-            def _(j):
-                scaled[j, i, ks] = (last[j, i, ks] - mean) * scale
 
     for n in range(len(coarse)):
         wait_others(t, n)
-    for at, group in enumerate(groups):
-        if group[0] is outer:
-            wait_i(t, group[3])
-        final_step(group)
-        if at > 0:
-            finish(groups[at - 1])
-        if at == len(groups) - 2:
-            wait_sent(STEPS - 2)
-    finish(groups[-1])
-
-    wait_sent(t)
+    count = len(coarse) if inner else 0
+    for group in groups[:count]:
+        inner_step(group)
+    for n in range(len(coarse)):
+        outer_ahead(n)
+    for group in groups[:count]:
+        finish(group)
+    wait_sent(STEPS - 2)
+    for n in range(len(final) - 1):
+        wait_i(t, n)
+        outer_step(n, own)
+        for off in range(1, rows):
+            stats_copy(off, groups[count + n]).start()
+        if n > 0:
+            finish(groups[count + n - 1])
+    wait_i(t, len(final) - 1)
+    outer_step(len(final) - 1, late)
+    if len(final) > 1:
+        finish(groups[-1])
     for group in groups:
         for off in range(1, rows):
             stats_copy(off, group).wait_send()
+    wait_sent(t)
+
+
+def planes_of(ni):
+    outer = tuple(range(ni)) if ni < 3 else (0, ni - 1)
+    return outer, tuple(i for i in range(ni) if i not in outer)
+
+
+def joined(nj, means, spreads):
+    count = len(means)
+    mean = sum(means[1:], means[0]) / count
+    spread = sum(spreads[1:], spreads[0])
+    for other in means:
+        spread = spread + nj * ((other - mean) * (other - mean))
+    return mean, lax.rsqrt(spread / (nj * count) + 0.0001)
 
 
 def write_out(near_anomaly, near_field, anomaly, field_end, sems):
@@ -346,6 +381,29 @@
         copy.wait()
 
 
+def write_late(before, near_field, late, *refs):
+    others, (anomaly, scaled, sems) = refs[:-3], refs[-3:]
+    nj, ni, nk, _ = near_field.shape
+    size = late.shape[2]
+    descending = lax.rem(lax.axis_index("slabs"), 2) == 0
+    start = pl.multiple_of(jnp.where(descending, 0, nk - size), TILE)
+    copies = []
+    for p, i in enumerate(planes_of(ni)[0]):
+        @pl.loop(0, size // TILE)
+        def _(b):
+            ks = pl.ds(pl.multiple_of(b * TILE, TILE), TILE)
+            ms = pl.ds(pl.multiple_of(start + b * TILE, TILE), TILE)
+            stats = (late,) + others
+            mean, scale = joined(nj, [of[0, p, ks] for of in stats], [of[1, p, ks] for of in stats])
+            for j in range(nj):
+                scaled[p, j, ks] = (near_field[j, i, ms] - mean) * scale
+
+        copies.append(pltpu.make_async_copy(scaled.at[p], anomaly.at[:, i, pl.ds(start, size)], sems.at[p]))
+        copies[-1].start()
+    for copy in copies:
+        copy.wait()
+
+
 def parts_of(nk):
     half = nk // 2 if nk % (2 * TILE) == 0 else nk
     coarse = (half,) * (nk // half)
@@ -367,12 +425,14 @@
     peers = max(sizes[0] - 1, 1)
     whole = pltpu.VMEM(field_values.shape, field_values.dtype)
     near = pl.BlockSpec(memory_space=pltpu.VMEM)
+    outer = len(planes_of(ni)[0])
+    small = (2, outer, parts[-1][-1], levels)
     anywhere = pl.BlockSpec(memory_space=pl.ANY)
-    results = pl.pallas_call(
+    scaled, last, late = pl.pallas_call(
         functools.partial(kernel, sizes, coarse, parts),
-        out_shape=(whole, whole),
+        out_shape=(whole, whole, pltpu.VMEM(small, jnp.float32)),
         in_specs=[anywhere] * 3,
-        out_specs=(near, near),
+        out_specs=(near, near, near),
         scratch_shapes=[
             pltpu.VMEM((STEPS, nj + 2, ni + 2, nk + 2 * TILE, levels), jnp.float32),
             pltpu.VMEM((nj, ni, nk, levels), jnp.float32),
@@ -394,17 +454,32 @@
         ),
         name="heat_steps",
     )(field_values, conductance, source)
+    n = sizes[0]
+    others = [lax.ppermute(late, "rows", [(r, (r + off) % n) for r in range(n)]) for off in range(1, n)]
     there = jax.ShapeDtypeStruct(field_values.shape, field_values.dtype)
     pieces = PIECES if nj % PIECES == 0 else 1
-    return pl.pallas_call(
+    size = nj * ni * nk * levels
+    anomaly, field_end = pl.pallas_call(
         write_out,
         out_shape=(there, there),
         in_specs=[near] * 2,
         out_specs=(anywhere, anywhere),
         scratch_shapes=[pltpu.SemaphoreType.DMA((2, pieces))],
         compiler_params=pltpu.CompilerParams(vmem_limit_bytes=1024 * 1024),
+        cost_estimate=pl.CostEstimate(flops=0, bytes_accessed=16 * size, transcendentals=0),
         name="write_out",
-    )(*results)
+    )(scaled, last)
+    anomaly = pl.pallas_call(
+        write_late,
+        out_shape=there,
+        in_specs=[anywhere] + [near] * (2 + len(others)),
+        out_specs=anywhere,
+        input_output_aliases={0: 0},
+        scratch_shapes=[pltpu.VMEM((outer, nj) + small[2:], jnp.float32), pltpu.SemaphoreType.DMA((outer,))],
+        compiler_params=pltpu.CompilerParams(vmem_limit_bytes=2 * 1024 * 1024),
+        name="write_late",
+    )(anomaly, last, late, *others)
+    return anomaly, field_end
 
 
 def solution(mesh):

time: 103 us -> 102 us (level)
  Pallas kernels: 102 us -> 99.5 us
  starting transfers between devices: 0 us -> 1.58 us
    pallas_call x1, Pallas kernels: 98.4 us -> 95.2 us  [on_device(): pl.pallas_call(functools.partial(kernel, sizes, coarse, parts), out_shape...]
    ppermute x0 -> x1, starting transfers between devices: none -> 1.58 us  [on_device(): lax.ppermute(late, 'rows', [(r, (r + off) % n) for r in range(n)])]
  transfers between devices with their start and end apart: 0 -> 1, of which waited for: 0 -> 0; matrix products, arithmetic and copies ran while one was open for 0% -> 0% of each run, Pallas kernels for 0% -> 3%
where the time goes in v3:
time: 102 us
  Pallas kernels  99.5 us (98%)
  starting transfers between devices  1.58 us (2%)
    pallas_call x1, Pallas kernels, on_device(): pl.pallas_call(functools.partial(kernel, sizes, coarse, parts), out_shape...  95.2 us
    pallas_call x1, Pallas kernels, on_device(): pl.pallas_call(write_out, out_shape=(there, there), in_specs=[near] * 2,...  3.36 us
  transfers between devices with their start and end apart: 1, of which 0 were waited for; matrix products, arithmetic and copies ran while one was open for 0% of the time, Pallas kernels for 3%

profile of v3, /device:TPU:0, one launch (start us, length us, event | category | flops | bytes accessed | tf_op | source)
XLA Modules:
  0.0 101.8 jit_solution(11681069542950431207)
XLA Ops:
  0.6 95.2 %heat_steps.1 = (f32[16,4,128,128]{3,2,1,0:T(8,128)S(1)}, f32[16,4,128,128]{3,2,1,0:T(8,128)S(1)}, f32[2,2,32,128]{3,2,1,0:T(8,128)S(1)}) custom-call(f32[16,4,128,128]{3,2,1,0:T(8,128)} %field.1, f32[16,4,128,128]{3,2,1,0:T(8,128)} %conductance.1, f32[16,4,128,128]{3,2,1,0:T(8,128)} %source.1), custom_call_target="tpu_custom_call" | custom-call | tf_op jit(solution)/shard_map/heat_steps/pallas_call | solution.py:431
  95.9 1.6 %collective-permute-start = (f32[2,2,32,128]{3,2,1,0:T(8,128)S(1)}, f32[2,2,32,128]{3,2,1,0:T(8,128)S(1)}, u32[]{:S(2)}, u32[]{:S(2)}) collective-permute-start(f32[2,2,32,128]{3,2,1,0:T(8,128)S(1)} %get-tuple-element.10.late), channel_id=1, source_target_pairs={{0,16},{16,0},{1,17},{17,1},{2,18},{18,2},{3,19},{19,3},{4,20},{20... | collective-permute-start | bytes 196616 | tf_op jit(solution)/shard_map/ppermute | solution.py:458
  97.4 3.4 %write_out.1 = (f32[16,4,128,128]{3,2,1,0:T(8,128)}, f32[16,4,128,128]{3,2,1,0:T(8,128)}) custom-call(f32[16,4,128,128]{3,2,1,0:T(8,128)S(1)} %get-tuple-element.7.near_anomaly, f32[16,4,128,128]{3,2,1,0:T(8,128)S(1)} %get-tuple-element.8.near_field), custom_call_target="tpu_custom_call" | custom-call | bytes 16777216 | tf_op jit(solution)/shard_map/write_out/pallas_call | solution.py:462
  100.8 0.0 collective-permute-done.refs_0_
  100.8 0.9 write_late.1
Async XLA Ops:
  95.9 5.0 %collective-permute-start = (f32[2,2,32,128]{3,2,1,0:T(8,128)S(1)}, f32[2,2,32,128]{3,2,1,0:T(8,128)S(1)}, u32[]{:S(2)}, u32[]{:S(2)}) collective-permute-start(f32[2,2,32,128]{3,2,1,0:T(8,128)S(1)} %get-tuple-element.10.late), channel_id=1, source_target_pairs={{0,16},{16,0},{1,17},{17,1},{2,18},{18,2},{3,19},{19,3},{4,20},{20... | collective-permute-start | bytes 196616 | tf_op jit(solution)/shard_map/ppermute | solution.py:458

commit v4 on v3

--- a/solution.py
+++ b/solution.py
@@ -38,12 +38,32 @@
     first_core = lax.rem(lax.axis_index("trial"), 2) == 0
     descending = lax.rem(slab, 2) == 0
 
+    def start_of(of, n):
+        before, size = sum(of[:n]), of[n]
+        return pl.multiple_of(jnp.where(descending, nk - before - size, before), TILE)
+
+    outer, inner = planes_of(ni)
+
+    def load(planes, ks, sem):
+        inside = pl.ds(ks.start + TILE, ks.size)
+        return pltpu.make_async_copy(
+            field.at[:, pl.ds(planes[0], len(planes)), ks],
+            u.at[0, pl.ds(1, nj), pl.ds(planes[0] + 1, len(planes)), inside], load_sem.at[sem],
+        )
+
+    early = [
+        [load((i,), pl.ds(start_of(coarse, n), coarse[n]), n * len(outer) + p) for p, i in enumerate(outer)]
+        for n in range(len(coarse))
+    ]
+    used = len(coarse) * len(outer)
     loads = [
-        pltpu.make_async_copy(field, u.at[0, pl.ds(1, nj), pl.ds(1, ni), pl.ds(TILE, nk)], load_sem.at[0]),
-        pltpu.make_async_copy(conductance, cond, load_sem.at[1]),
-        pltpu.make_async_copy(source, src, load_sem.at[2]),
+        pltpu.make_async_copy(conductance, cond, load_sem.at[used]),
+        pltpu.make_async_copy(source, src, load_sem.at[used + 1]),
     ]
-    loads[0].start()
+    rest = [load(inner, pl.ds(0, nk), used + 2)] if inner else []
+    for part in early:
+        for copy in part:
+            copy.start()
 
     barrier = pltpu.get_barrier_semaphore()
     expected = rows - 1
@@ -58,10 +78,6 @@
 
     pl.semaphore_wait(barrier, expected)
 
-    def start_of(of, n):
-        before, size = sum(of[:n]), of[n]
-        return pl.multiple_of(jnp.where(descending, nk - before - size, before), TILE)
-
     def edges_of(n):
         first, final = n == 0, n == len(coarse) - 1
         low = jnp.where(descending, final, first)
@@ -71,16 +87,16 @@
     def face(side, t, n, first):
         of = parts[t] if side[0] == "i" else coarse
         k0, kq = start_of(of, n), of[n]
-        inner = pl.ds(pl.multiple_of(TILE + k0, TILE), kq)
+        inside = pl.ds(pl.multiple_of(TILE + k0, TILE), kq)
         js, is_ = pl.ds(1, nj), pl.ds(1, ni)
         if side[0] == "i":
             here, there = (1, ni + 1) if side == "i-" else (ni, 0)
-            dst = u.at[t, js, there, inner]
-            start = field.at[:, here - 1, pl.ds(k0, kq)] if first else u.at[t, js, here, inner]
+            dst = u.at[t, js, there, inside]
+            start = u.at[t, js, here, inside]
         else:
             here, there = (1, nj + 1) if side == "j-" else (nj, 0)
-            dst = u.at[t, there, is_, inner]
-            start = field.at[here - 1, :, pl.ds(k0, kq)] if first else u.at[t, here, is_, inner]
+            dst = u.at[t, there, is_, inside]
+            start = field.at[here - 1, :, pl.ds(k0, kq)] if first else u.at[t, here, is_, inside]
         d = 0 if side[1] == "-" else 1
         sent, received = (send_sem, recv_sem) if side[0] == "i" else (jsend_sem, jrecv_sem)
         return pltpu.make_async_remote_copy(
@@ -103,13 +119,14 @@
         low, done = sum(coarse[:n]), sum(coarse[:n + 1])
         return [m for m in range(len(parts[t])) if low <= sum(parts[t][:m]) < done]
 
-    def send_faces(t, n, first):
+    def send_i(t, n):
         for side in ("i-", "i+"):
             @pl.when(has[side])
             def _():
                 for m in fine_of(t, n):
-                    face(side, t, m, first).start()
-
+                    face(side, t, m, False).start()
+
+    def send_others(t, n, first):
         for side in ("j-", "j+"):
             @pl.when(has[side])
             def _():
@@ -168,10 +185,15 @@
                 kface(side, t, False).wait_send()
 
     for n in range(len(coarse)):
-        send_faces(0, n, True)
-
-    loads[1].start()
-    loads[2].start()
+        for copy in early[n]:
+            copy.wait()
+        send_i(0, n)
+    for n in range(len(coarse)):
+        send_others(0, n, True)
+    for copy in rest:
+        copy.start()
+    for copy in loads:
+        copy.start()
 
     def zero_plane(t, j, i):
         u[t, j, i, pl.ds(TILE, nk)] = jnp.zeros((nk, u.shape[-1]), u.dtype)
@@ -199,8 +221,8 @@
                     for i in range(ni):
                         u[t, j + 1, i + 1, pl.ds(k, TILE)] = jnp.zeros((TILE, u.shape[-1]), u.dtype)
 
-    for load in loads:
-        load.wait()
+    for copy in rest + loads:
+        copy.wait()
 
     def stencil(t, j, i, k0, kq, skip=(False, False)):
         inner = pl.ds(pl.multiple_of(TILE + k0, TILE), kq)
@@ -234,7 +256,8 @@
             def _():
                 pl.delay(PAUSE)
 
-        send_faces(t + 1, n, False)
+        send_i(t + 1, n)
+        send_others(t + 1, n, False)
 
     for t in range(STEPS - 1):
         for n in range(len(coarse)):
@@ -244,7 +267,6 @@
 
     t = STEPS - 1
     final = parts[t]
-    outer, inner = planes_of(ni)
     groups = [(inner, len(outer), coarse, n, n) for n in range(len(coarse))] if inner else []
     groups += [(outer, 0, final, n, len(coarse) + n) for n in range(len(final) - 1)]
 
@@ -439,7 +461,7 @@
             pltpu.VMEM((nj, ni, nk, levels), jnp.float32),
             pltpu.VMEM((2, ni, nk, levels), jnp.float32),
             pltpu.VMEM((peers, 2, ni, nk, levels), jnp.float32),
-            pltpu.SemaphoreType.DMA((3,)),
+            pltpu.SemaphoreType.DMA((len(coarse) * outer + 3,)),
             pltpu.SemaphoreType.DMA((2, STEPS, most)),
             pltpu.SemaphoreType.DMA((2, STEPS, most)),
             pltpu.SemaphoreType.DMA((2, STEPS, len(coarse))),

time: 102 us -> 102 us (level)
  no operation moved by 1% of the time
where the time goes in v4:
time: 102 us
  Pallas kernels  99.3 us (97%)
  starting transfers between devices  1.58 us (2%)
    pallas_call x1, Pallas kernels, on_device(): pl.pallas_call(functools.partial(kernel, sizes, coarse, parts), out_shape...  95 us
    pallas_call x1, Pallas kernels, on_device(): pl.pallas_call(write_out, out_shape=(there, there), in_specs=[near] * 2,...  3.36 us
  transfers between devices with their start and end apart: 1, of which 0 were waited for; matrix products, arithmetic and copies ran while one was open for 0% of the time, Pallas kernels for 3%

profile of v4, /device:TPU:0, one launch (start us, length us, event | category | flops | bytes accessed | tf_op | source)
XLA Modules:
  0.0 101.6 jit_solution(13808751067916362286)
XLA Ops:
  0.6 95.0 %heat_steps.1 = (f32[16,4,128,128]{3,2,1,0:T(8,128)S(1)}, f32[16,4,128,128]{3,2,1,0:T(8,128)S(1)}, f32[2,2,32,128]{3,2,1,0:T(8,128)S(1)}) custom-call(f32[16,4,128,128]{3,2,1,0:T(8,128)} %field.1, f32[16,4,128,128]{3,2,1,0:T(8,128)} %conductance.1, f32[16,4,128,128]{3,2,1,0:T(8,128)} %source.1), custom_call_target="tpu_custom_call" | custom-call | tf_op jit(solution)/shard_map/heat_steps/pallas_call | solution.py:453
  95.7 1.6 %collective-permute-start = (f32[2,2,32,128]{3,2,1,0:T(8,128)S(1)}, f32[2,2,32,128]{3,2,1,0:T(8,128)S(1)}, u32[]{:S(2)}, u32[]{:S(2)}) collective-permute-start(f32[2,2,32,128]{3,2,1,0:T(8,128)S(1)} %get-tuple-element.10.late), channel_id=1, source_target_pairs={{0,16},{16,0},{1,17},{17,1},{2,18},{18,2},{3,19},{19,3},{4,20},{20... | collective-permute-start | bytes 196616 | tf_op jit(solution)/shard_map/ppermute | solution.py:480
  97.3 3.4 %write_out.1 = (f32[16,4,128,128]{3,2,1,0:T(8,128)}, f32[16,4,128,128]{3,2,1,0:T(8,128)}) custom-call(f32[16,4,128,128]{3,2,1,0:T(8,128)S(1)} %get-tuple-element.7.near_anomaly, f32[16,4,128,128]{3,2,1,0:T(8,128)S(1)} %get-tuple-element.8.near_field), custom_call_target="tpu_custom_call" | custom-call | bytes 16777216 | tf_op jit(solution)/shard_map/write_out/pallas_call | solution.py:484
  100.6 0.0 collective-permute-done.refs_0_
  100.7 0.9 write_late.1
Async XLA Ops:
  95.7 5.0 %collective-permute-start = (f32[2,2,32,128]{3,2,1,0:T(8,128)S(1)}, f32[2,2,32,128]{3,2,1,0:T(8,128)S(1)}, u32[]{:S(2)}, u32[]{:S(2)}) collective-permute-start(f32[2,2,32,128]{3,2,1,0:T(8,128)S(1)} %get-tuple-element.10.late), channel_id=1, source_target_pairs={{0,16},{16,0},{1,17},{17,1},{2,18},{18,2},{3,19},{19,3},{4,20},{20... | collective-permute-start | bytes 196616 | tf_op jit(solution)/shard_map/ppermute | solution.py:480

commit v5 on v3

--- a/solution.py
+++ b/solution.py
@@ -12,14 +12,14 @@
 PIECES = 4
 FINE = (4,)
 YIELD = 1
-PAUSE = 2000
+PAUSE = 1000
 MESH = pl.DeviceIdType.MESH
 
 
 def kernel(
     sizes, coarse, parts, field, conductance, source, scaled, last, late,
     u, cond, src, own, others,
-    load_sem, send_sem, recv_sem, jsend_sem, jrecv_sem, ksend_sem, krecv_sem, ssend_sem, srecv_sem,
+    load_sem, send_sem, recv_sem, jsend_sem, jrecv_sem, ksend_sem, krecv_sem, ssend_sem, srecv_sem, ready_sem,
 ):
     rows, cols, slabs = sizes
     nj, ni, nk, _ = field.shape
@@ -38,29 +38,47 @@
     first_core = lax.rem(lax.axis_index("trial"), 2) == 0
     descending = lax.rem(slab, 2) == 0
 
+    def start_of(of, n):
+        before, size = sum(of[:n]), of[n]
+        return pl.multiple_of(jnp.where(descending, nk - before - size, before), TILE)
+
+    outer, inner = planes_of(ni)
     loads = [
         pltpu.make_async_copy(field, u.at[0, pl.ds(1, nj), pl.ds(1, ni), pl.ds(TILE, nk)], load_sem.at[0]),
         pltpu.make_async_copy(conductance, cond, load_sem.at[1]),
         pltpu.make_async_copy(source, src, load_sem.at[2]),
     ]
-    loads[0].start()
 
     barrier = pltpu.get_barrier_semaphore()
-    expected = rows - 1
     for off in range(1, rows):
-        pl.semaphore_signal(barrier, inc=1, device_id={"rows": lax.rem(row + off, rows)}, device_id_type=MESH)
-    for side in ("i-", "i+", "k-", "k+"):
-        expected = expected + jnp.where(has[side], 1, 0)
-
-        @pl.when(has[side])
-        def _():
-            pl.semaphore_signal(barrier, inc=1, device_id=to[side], device_id_type=MESH)
-
-    pl.semaphore_wait(barrier, expected)
-
-    def start_of(of, n):
-        before, size = sum(of[:n]), of[n]
-        return pl.multiple_of(jnp.where(descending, nk - before - size, before), TILE)
+        @pl.when(row + off < rows)
+        def _():
+            pl.semaphore_signal(barrier, inc=1, device_id={"rows": jnp.minimum(row + off, rows - 1)}, device_id_type=MESH)
+
+    expected = row
+    for side in ("i", "k"):
+        expected = expected + jnp.where(has[side + "-"], 1, 0)
+
+        @pl.when(has[side + "+"])
+        def _():
+            pl.semaphore_signal(barrier, inc=1, device_id=to[side + "+"], device_id_type=MESH)
+
+
+    @pl.when(expected > 0)
+    def _():
+        pl.semaphore_wait(barrier, expected)
+
+    for side, at in (("i", rows - 1), ("k", rows)):
+        @pl.when(has[side + "-"])
+        def _():
+            pl.semaphore_signal(ready_sem.at[at], inc=1, device_id=to[side + "-"], device_id_type=MESH)
+
+    for off in range(1, rows):
+        @pl.when(row >= off)
+        def _():
+            pl.semaphore_signal(
+                ready_sem.at[off - 1], inc=1, device_id={"rows": jnp.maximum(row - off, 0)}, device_id_type=MESH
+            )
 
     def edges_of(n):
         first, final = n == 0, n == len(coarse) - 1
@@ -71,16 +89,16 @@
     def face(side, t, n, first):
         of = parts[t] if side[0] == "i" else coarse
         k0, kq = start_of(of, n), of[n]
-        inner = pl.ds(pl.multiple_of(TILE + k0, TILE), kq)
+        inside = pl.ds(pl.multiple_of(TILE + k0, TILE), kq)
         js, is_ = pl.ds(1, nj), pl.ds(1, ni)
         if side[0] == "i":
             here, there = (1, ni + 1) if side == "i-" else (ni, 0)
-            dst = u.at[t, js, there, inner]
-            start = field.at[:, here - 1, pl.ds(k0, kq)] if first else u.at[t, js, here, inner]
+            dst = u.at[t, js, there, inside]
+            start = field.at[:, here - 1, pl.ds(k0, kq)] if first else u.at[t, js, here, inside]
         else:
             here, there = (1, nj + 1) if side == "j-" else (nj, 0)
-            dst = u.at[t, there, is_, inner]
-            start = field.at[here - 1, :, pl.ds(k0, kq)] if first else u.at[t, here, is_, inner]
+            dst = u.at[t, there, is_, inside]
+            start = field.at[here - 1, :, pl.ds(k0, kq)] if first else u.at[t, here, is_, inside]
         d = 0 if side[1] == "-" else 1
         sent, received = (send_sem, recv_sem) if side[0] == "i" else (jsend_sem, jrecv_sem)
         return pltpu.make_async_remote_copy(
@@ -103,13 +121,14 @@
         low, done = sum(coarse[:n]), sum(coarse[:n + 1])
         return [m for m in range(len(parts[t])) if low <= sum(parts[t][:m]) < done]
 
-    def send_faces(t, n, first):
-        for side in ("i-", "i+"):
+    def send_i(t, n, first, towards=("i-", "i+")):
+        for side in towards:
             @pl.when(has[side])
             def _():
                 for m in fine_of(t, n):
                     face(side, t, m, first).start()
 
+    def send_others(t, n, first):
         for side in ("j-", "j+"):
             @pl.when(has[side])
             def _():
@@ -168,10 +187,28 @@
                 kface(side, t, False).wait_send()
 
     for n in range(len(coarse)):
-        send_faces(0, n, True)
-
-    loads[1].start()
-    loads[2].start()
+        send_i(0, n, True, ("i-",))
+
+    @pl.when(has["i+"])
+    def _():
+        pl.semaphore_wait(ready_sem.at[rows - 1], 1)
+
+    for n in range(len(coarse)):
+        send_i(0, n, True, ("i+",))
+
+    @pl.when(has["k+"])
+    def _():
+        pl.semaphore_wait(ready_sem.at[rows], 1)
+
+    for off in range(1, rows):
+        @pl.when(row + off < rows)
+        def _():
+            pl.semaphore_wait(ready_sem.at[off - 1], 1)
+
+    for n in range(len(coarse)):
+        send_others(0, n, True)
+    for copy in loads:
+        copy.start()
 
     def zero_plane(t, j, i):
         u[t, j, i, pl.ds(TILE, nk)] = jnp.zeros((nk, u.shape[-1]), u.dtype)
@@ -199,8 +236,8 @@
                     for i in range(ni):
                         u[t, j + 1, i + 1, pl.ds(k, TILE)] = jnp.zeros((TILE, u.shape[-1]), u.dtype)
 
-    for load in loads:
-        load.wait()
+    for copy in loads:
+        copy.wait()
 
     def stencil(t, j, i, k0, kq, skip=(False, False)):
         inner = pl.ds(pl.multiple_of(TILE + k0, TILE), kq)
@@ -234,7 +271,8 @@
             def _():
                 pl.delay(PAUSE)
 
-        send_faces(t + 1, n, False)
+        send_i(t + 1, n, False)
+        send_others(t + 1, n, False)
 
     for t in range(STEPS - 1):
         for n in range(len(coarse)):
@@ -244,7 +282,6 @@
 
     t = STEPS - 1
     final = parts[t]
-    outer, inner = planes_of(ni)
     groups = [(inner, len(outer), coarse, n, n) for n in range(len(coarse))] if inner else []
     groups += [(outer, 0, final, n, len(coarse) + n) for n in range(len(final) - 1)]
 
@@ -448,6 +485,7 @@
             pltpu.SemaphoreType.DMA((2, STEPS)),
             pltpu.SemaphoreType.DMA((peers, groups)),
             pltpu.SemaphoreType.DMA((peers, groups)),
+            pltpu.SemaphoreType.REGULAR((sizes[0] + 1,)),
         ],
         compiler_params=pltpu.CompilerParams(
             collective_id=0, has_side_effects=True, vmem_limit_bytes=52 * 1024 * 1024

time: 102 us -> 101 us (level)
  Pallas kernels: 99.5 us -> 98.2 us
    pallas_call x1, Pallas kernels: 95.2 us -> 93.9 us  [on_device(): pl.pallas_call(functools.partial(kernel, sizes, coarse, parts), out_shape...]
where the time goes in v5:
time: 101 us
  Pallas kernels  98.2 us (97%)
  starting transfers between devices  2 us (2%)
    pallas_call x1, Pallas kernels, on_device(): pl.pallas_call(functools.partial(kernel, sizes, coarse, parts), out_shape...  93.9 us
    pallas_call x1, Pallas kernels, on_device(): pl.pallas_call(write_out, out_shape=(there, there), in_specs=[near] * 2,...  3.36 us
  transfers between devices with their start and end apart: 1, of which 0 were waited for; matrix products, arithmetic and copies ran while one was open for 0% of the time, Pallas kernels for 3%

profile of v5, /device:TPU:0, one launch (start us, length us, event | category | flops | bytes accessed | tf_op | source)
XLA Modules:
  0.0 100.8 jit_solution(4487394694932060107)
XLA Ops:
  0.6 93.9 %heat_steps.1 = (f32[16,4,128,128]{3,2,1,0:T(8,128)S(1)}, f32[16,4,128,128]{3,2,1,0:T(8,128)S(1)}, f32[2,2,32,128]{3,2,1,0:T(8,128)S(1)}) custom-call(f32[16,4,128,128]{3,2,1,0:T(8,128)} %field.1, f32[16,4,128,128]{3,2,1,0:T(8,128)} %conductance.1, f32[16,4,128,128]{3,2,1,0:T(8,128)} %source.1), custom_call_target="tpu_custom_call" | custom-call | tf_op jit(solution)/shard_map/heat_steps/pallas_call | solution.py:468
  94.5 2.0 %collective-permute-start = (f32[2,2,32,128]{3,2,1,0:T(8,128)S(1)}, f32[2,2,32,128]{3,2,1,0:T(8,128)S(1)}, u32[]{:S(2)}, u32[]{:S(2)}) collective-permute-start(f32[2,2,32,128]{3,2,1,0:T(8,128)S(1)} %get-tuple-element.10.late), channel_id=1, source_target_pairs={{0,16},{16,0},{1,17},{17,1},{2,18},{18,2},{3,19},{19,3},{4,20},{20... | collective-permute-start | bytes 196616 | tf_op jit(solution)/shard_map/ppermute | solution.py:496
  96.5 3.4 %write_out.1 = (f32[16,4,128,128]{3,2,1,0:T(8,128)}, f32[16,4,128,128]{3,2,1,0:T(8,128)}) custom-call(f32[16,4,128,128]{3,2,1,0:T(8,128)S(1)} %get-tuple-element.7.near_anomaly, f32[16,4,128,128]{3,2,1,0:T(8,128)S(1)} %get-tuple-element.8.near_field), custom_call_target="tpu_custom_call" | custom-call | bytes 16777216 | tf_op jit(solution)/shard_map/write_out/pallas_call | solution.py:500
  99.9 0.0 collective-permute-done.refs_0_
  99.9 0.9 write_late.1
Async XLA Ops:
  94.5 5.4 %collective-permute-start = (f32[2,2,32,128]{3,2,1,0:T(8,128)S(1)}, f32[2,2,32,128]{3,2,1,0:T(8,128)S(1)}, u32[]{:S(2)}, u32[]{:S(2)}) collective-permute-start(f32[2,2,32,128]{3,2,1,0:T(8,128)S(1)} %get-tuple-element.10.late), channel_id=1, source_target_pairs={{0,16},{16,0},{1,17},{17,1},{2,18},{18,2},{3,19},{19,3},{4,20},{20... | collective-permute-start | bytes 196616 | tf_op jit(solution)/shard_map/ppermute | solution.py:496

commit v6 on v5

--- a/solution.py
+++ b/solution.py
@@ -12,7 +12,7 @@
 PIECES = 4
 FINE = (4,)
 YIELD = 1
-PAUSE = 1000
+PAUSE = 1200
 MESH = pl.DeviceIdType.MESH
 
 
@@ -404,16 +404,27 @@
     return mean, lax.rsqrt(spread / (nj * count) + 0.0001)
 
 
-def write_out(near_anomaly, near_field, anomaly, field_end, sems):
+def late_start(nk, size):
+    descending = lax.rem(lax.axis_index("slabs"), 2) == 0
+    return pl.multiple_of(jnp.where(descending, 0, nk - size), TILE)
+
+
+def write_out(late, near_anomaly, near_field, anomaly, field_end, sems):
+    nj, ni, nk, _ = near_field.shape
+    pieces = sems.shape[1]
+    depth = nj // pieces
+    outer, inner = planes_of(ni)
+    places = [(0, (pl.ds(piece * depth, depth),)) for piece in range(pieces)]
+    if inner:
+        places += [(1, (pl.ds(piece * depth, depth), pl.ds(inner[0], len(inner)))) for piece in range(pieces)]
+    if late < nk:
+        early = pl.ds(pl.multiple_of(jnp.where(late_start(nk, late) == 0, late, 0), TILE), nk - late)
+        places += [(1, (slice(None), i, early)) for i in outer]
     copies = []
-    for which, (start, dst) in enumerate(((near_field, field_end), (near_anomaly, anomaly))):
-        pieces = sems.shape[1]
-        depth = start.shape[0] // pieces
-        for piece in range(pieces):
-            js = pl.ds(piece * depth, depth)
-            copies.append(pltpu.make_async_copy(start.at[js], dst.at[js], sems.at[which, piece]))
-    for copy in copies:
-        copy.start()
+    for at, (which, place) in enumerate(places):
+        start, dst = ((near_field, field_end), (near_anomaly, anomaly))[which]
+        copies.append(pltpu.make_async_copy(start.at[place], dst.at[place], sems.at[at // pieces, at % pieces]))
+        copies[-1].start()
     for copy in copies:
         copy.wait()
 
@@ -422,21 +433,17 @@
     others, (anomaly, scaled, sems) = refs[:-3], refs[-3:]
     nj, ni, nk, _ = near_field.shape
     size = late.shape[2]
-    descending = lax.rem(lax.axis_index("slabs"), 2) == 0
-    start = pl.multiple_of(jnp.where(descending, 0, nk - size), TILE)
+    start = late_start(nk, size)
     copies = []
-    for p, i in enumerate(planes_of(ni)[0]):
-        @pl.loop(0, size // TILE)
-        def _(b):
-            ks = pl.ds(pl.multiple_of(b * TILE, TILE), TILE)
-            ms = pl.ds(pl.multiple_of(start + b * TILE, TILE), TILE)
+    for b in range(size // TILE):
+        ks, ms = pl.ds(b * TILE, TILE), pl.ds(pl.multiple_of(start + b * TILE, TILE), TILE)
+        for p, i in enumerate(planes_of(ni)[0]):
             stats = (late,) + others
             mean, scale = joined(nj, [of[0, p, ks] for of in stats], [of[1, p, ks] for of in stats])
             for j in range(nj):
                 scaled[p, j, ks] = (near_field[j, i, ms] - mean) * scale
-
-        copies.append(pltpu.make_async_copy(scaled.at[p], anomaly.at[:, i, pl.ds(start, size)], sems.at[p]))
-        copies[-1].start()
+            copies.append(pltpu.make_async_copy(scaled.at[p, :, ks], anomaly.at[:, i, ms], sems.at[p, b]))
+            copies[-1].start()
     for copy in copies:
         copy.wait()
 
@@ -498,11 +505,11 @@
     pieces = PIECES if nj % PIECES == 0 else 1
     size = nj * ni * nk * levels
     anomaly, field_end = pl.pallas_call(
-        write_out,
+        functools.partial(write_out, small[2]),
         out_shape=(there, there),
         in_specs=[near] * 2,
         out_specs=(anywhere, anywhere),
-        scratch_shapes=[pltpu.SemaphoreType.DMA((2, pieces))],
+        scratch_shapes=[pltpu.SemaphoreType.DMA((2 + -(-outer // pieces), pieces))],
         compiler_params=pltpu.CompilerParams(vmem_limit_bytes=1024 * 1024),
         cost_estimate=pl.CostEstimate(flops=0, bytes_accessed=16 * size, transcendentals=0),
         name="write_out",
@@ -513,7 +520,7 @@
         in_specs=[anywhere] + [near] * (2 + len(others)),
         out_specs=anywhere,
         input_output_aliases={0: 0},
-        scratch_shapes=[pltpu.VMEM((outer, nj) + small[2:], jnp.float32), pltpu.SemaphoreType.DMA((outer,))],
+        scratch_shapes=[pltpu.VMEM((outer, nj) + small[2:], jnp.float32), pltpu.SemaphoreType.DMA((outer, small[2] // TILE))],
         compiler_params=pltpu.CompilerParams(vmem_limit_bytes=2 * 1024 * 1024),
         name="write_late",
     )(anomaly, last, late, *others)

time: 101 us -> 101 us (level)
  no operation moved by 1% of the time
where the time goes in v6:
time: 101 us; the launch traced here: 100 us
  Pallas kernels  97.8 us (97%)
  starting transfers between devices  2 us (2%)
    pallas_call x1, Pallas kernels, on_device(): pl.pallas_call(functools.partial(kernel, sizes, coarse, parts), out_shape...  93.7 us
    pallas_call x1, Pallas kernels, on_device(): pl.pallas_call(functools.partial(write_out, small[2]), out_shape=(there,...  3.23 us
  transfers between devices with their start and end apart: 1, of which 0 were waited for; matrix products, arithmetic and copies ran while one was open for 0% of the time, Pallas kernels for 3%

profile of v6, /device:TPU:0, one launch (start us, length us, event | category | flops | bytes accessed | tf_op | source)
XLA Modules:
  0.0 100.4 jit_solution(15933515927443713661)
XLA Ops:
  0.6 93.7 %heat_steps.1 = (f32[16,4,128,128]{3,2,1,0:T(8,128)S(1)}, f32[16,4,128,128]{3,2,1,0:T(8,128)S(1)}, f32[2,2,32,128]{3,2,1,0:T(8,128)S(1)}) custom-call(f32[16,4,128,128]{3,2,1,0:T(8,128)} %field.1, f32[16,4,128,128]{3,2,1,0:T(8,128)} %conductance.1, f32[16,4,128,128]{3,2,1,0:T(8,128)} %source.1), custom_call_target="tpu_custom_call" | custom-call | tf_op jit(solution)/shard_map/heat_steps/pallas_call | solution.py:475
  94.3 2.0 %collective-permute-start = (f32[2,2,32,128]{3,2,1,0:T(8,128)S(1)}, f32[2,2,32,128]{3,2,1,0:T(8,128)S(1)}, u32[]{:S(2)}, u32[]{:S(2)}) collective-permute-start(f32[2,2,32,128]{3,2,1,0:T(8,128)S(1)} %get-tuple-element.10.late), channel_id=1, source_target_pairs={{0,16},{16,0},{1,17},{17,1},{2,18},{18,2},{3,19},{19,3},{4,20},{20... | collective-permute-start | bytes 196616 | tf_op jit(solution)/shard_map/ppermute | solution.py:503
  96.3 3.2 %write_out.1 = (f32[16,4,128,128]{3,2,1,0:T(8,128)}, f32[16,4,128,128]{3,2,1,0:T(8,128)}) custom-call(f32[16,4,128,128]{3,2,1,0:T(8,128)S(1)} %get-tuple-element.7.near_anomaly, f32[16,4,128,128]{3,2,1,0:T(8,128)S(1)} %get-tuple-element.8.near_field), custom_call_target="tpu_custom_call" | custom-call | bytes 16777216 | tf_op jit(solution)/shard_map/write_out/pallas_call | solution.py:507
  99.5 0.0 collective-permute-done.refs_0_
  99.6 0.9 write_late.1
Async XLA Ops:
  94.3 5.2 %collective-permute-start = (f32[2,2,32,128]{3,2,1,0:T(8,128)S(1)}, f32[2,2,32,128]{3,2,1,0:T(8,128)S(1)}, u32[]{:S(2)}, u32[]{:S(2)}) collective-permute-start(f32[2,2,32,128]{3,2,1,0:T(8,128)S(1)} %get-tuple-element.10.late), channel_id=1, source_target_pairs={{0,16},{16,0},{1,17},{17,1},{2,18},{18,2},{3,19},{19,3},{4,20},{20... | collective-permute-start | bytes 196616 | tf_op jit(solution)/shard_map/ppermute | solution.py:503

commit v7 on v6

--- a/solution.py
+++ b/solution.py
@@ -12,7 +12,7 @@
 PIECES = 4
 FINE = (4,)
 YIELD = 1
-PAUSE = 1200
+PAUSE = 1000
 MESH = pl.DeviceIdType.MESH
 
 
@@ -380,10 +380,19 @@
             stats_copy(off, groups[count + n]).start()
         if n > 0:
             finish(groups[count + n - 1])
+    first_rows = row < rows // 2
+    if len(final) > 1:
+        @pl.when(jnp.logical_not(first_rows))
+        def _():
+            finish(groups[-1])
+
     wait_i(t, len(final) - 1)
     outer_step(len(final) - 1, late)
     if len(final) > 1:
-        finish(groups[-1])
+        @pl.when(first_rows)
+        def _():
+            finish(groups[-1])
+
     for group in groups:
         for off in range(1, rows):
             stats_copy(off, group).wait_send()

time: 101 us -> 101 us (level)
  no operation moved by 1% of the time
where the time goes in v7:
time: 101 us
  Pallas kernels  98 us (97%)
  starting transfers between devices  2 us (2%)
    pallas_call x1, Pallas kernels, on_device(): pl.pallas_call(functools.partial(kernel, sizes, coarse, parts), out_shape...  93.9 us
    pallas_call x1, Pallas kernels, on_device(): pl.pallas_call(functools.partial(write_out, small[2]), out_shape=(there,...  3.23 us
  transfers between devices with their start and end apart: 1, of which 0 were waited for; matrix products, arithmetic and copies ran while one was open for 0% of the time, Pallas kernels for 3%

profile of v7, /device:TPU:0, one launch (start us, length us, event | category | flops | bytes accessed | tf_op | source)
XLA Modules:
  0.0 100.6 jit_solution(6138145473385200901)
XLA Ops:
  0.6 93.9 %heat_steps.1 = (f32[16,4,128,128]{3,2,1,0:T(8,128)S(1)}, f32[16,4,128,128]{3,2,1,0:T(8,128)S(1)}, f32[2,2,32,128]{3,2,1,0:T(8,128)S(1)}) custom-call(f32[16,4,128,128]{3,2,1,0:T(8,128)} %field.1, f32[16,4,128,128]{3,2,1,0:T(8,128)} %conductance.1, f32[16,4,128,128]{3,2,1,0:T(8,128)} %source.1), custom_call_target="tpu_custom_call" | custom-call | tf_op jit(solution)/shard_map/heat_steps/pallas_call | solution.py:484
  94.5 2.0 %collective-permute-start = (f32[2,2,32,128]{3,2,1,0:T(8,128)S(1)}, f32[2,2,32,128]{3,2,1,0:T(8,128)S(1)}, u32[]{:S(2)}, u32[]{:S(2)}) collective-permute-start(f32[2,2,32,128]{3,2,1,0:T(8,128)S(1)} %get-tuple-element.10.late), channel_id=1, source_target_pairs={{0,16},{16,0},{1,17},{17,1},{2,18},{18,2},{3,19},{19,3},{4,20},{20... | collective-permute-start | bytes 196616 | tf_op jit(solution)/shard_map/ppermute | solution.py:512
  96.5 3.2 %write_out.1 = (f32[16,4,128,128]{3,2,1,0:T(8,128)}, f32[16,4,128,128]{3,2,1,0:T(8,128)}) custom-call(f32[16,4,128,128]{3,2,1,0:T(8,128)S(1)} %get-tuple-element.7.near_anomaly, f32[16,4,128,128]{3,2,1,0:T(8,128)S(1)} %get-tuple-element.8.near_field), custom_call_target="tpu_custom_call" | custom-call | bytes 16777216 | tf_op jit(solution)/shard_map/write_out/pallas_call | solution.py:516
  99.7 0.0 collective-permute-done.refs_0_
  99.8 0.9 write_late.1
Async XLA Ops:
  94.5 5.2 %collective-permute-start = (f32[2,2,32,128]{3,2,1,0:T(8,128)S(1)}, f32[2,2,32,128]{3,2,1,0:T(8,128)S(1)}, u32[]{:S(2)}, u32[]{:S(2)}) collective-permute-start(f32[2,2,32,128]{3,2,1,0:T(8,128)S(1)} %get-tuple-element.10.late), channel_id=1, source_target_pairs={{0,16},{16,0},{1,17},{17,1},{2,18},{18,2},{3,19},{19,3},{4,20},{20... | collective-permute-start | bytes 196616 | tf_op jit(solution)/shard_map/ppermute | solution.py:512

commit v8 on v7

--- a/solution.py
+++ b/solution.py
@@ -10,9 +10,10 @@
 STEPS = 4
 TILE = 8
 PIECES = 4
-FINE = (4,)
+FINE = (4, 3)
+LATE = 2
 YIELD = 1
-PAUSE = 1000
+PAUSE = 1300
 MESH = pl.DeviceIdType.MESH
 
 
@@ -282,8 +283,9 @@
 
     t = STEPS - 1
     final = parts[t]
+    prompt = len(final) - min(LATE, len(final))
     groups = [(inner, len(outer), coarse, n, n) for n in range(len(coarse))] if inner else []
-    groups += [(outer, 0, final, n, len(coarse) + n) for n in range(len(final) - 1)]
+    groups += [(outer, 0, final, n, len(coarse) + n) for n in range(prompt)]
 
     def stats_copy(off, group):
         planes, at, of, n, sem = group
@@ -331,7 +333,7 @@
                 for j in range(nj):
                     last[j, i, pl.ds(k, TILE)] = stencil(t, j, i, k, TILE, skip=(i == 0, i == ni - 1))
 
-    def outer_step(n, into):
+    def outer_step(n):
         @blocks(final, n)
         def _(k, b):
             ks, inside = pl.ds(k, TILE), pl.ds(pl.multiple_of(TILE + k, TILE), TILE)
@@ -341,10 +343,11 @@
                 for j in range(nj):
                     arrived = [u[t, j + 1, face, inside] for face in faces]
                     news.append(last[j, i, ks] + cond[j, i, ks] * sum(arrived[1:], arrived[0]))
-                if into is own:
+                if n < prompt:
                     own[0, p, ks], own[1, p, ks] = sums_of(news)
                 else:
-                    into[0, p, pl.ds(b, TILE)], into[1, p, pl.ds(b, TILE)] = sums_of(news)
+                    at = pl.ds(pl.multiple_of(k - late_start(nk, late.shape[2]), TILE), TILE)
+                    late[0, p, at], late[1, p, at] = sums_of(news)
                 for j in range(nj):
                     last[j, i, ks] = news[j]
 
@@ -373,22 +376,23 @@
     for group in groups[:count]:
         finish(group)
     wait_sent(STEPS - 2)
-    for n in range(len(final) - 1):
+    for n in range(prompt):
         wait_i(t, n)
-        outer_step(n, own)
+        outer_step(n)
         for off in range(1, rows):
             stats_copy(off, groups[count + n]).start()
         if n > 0:
             finish(groups[count + n - 1])
     first_rows = row < rows // 2
-    if len(final) > 1:
+    if prompt > 0:
         @pl.when(jnp.logical_not(first_rows))
         def _():
             finish(groups[-1])
 
-    wait_i(t, len(final) - 1)
-    outer_step(len(final) - 1, late)
-    if len(final) > 1:
+    for n in range(prompt, len(final)):
+        wait_i(t, n)
+        outer_step(n)
+    if prompt > 0:
         @pl.when(first_rows)
         def _():
             finish(groups[-1])
@@ -479,7 +483,7 @@
     whole = pltpu.VMEM(field_values.shape, field_values.dtype)
     near = pl.BlockSpec(memory_space=pltpu.VMEM)
     outer = len(planes_of(ni)[0])
-    small = (2, outer, parts[-1][-1], levels)
+    small = (2, outer, sum(parts[-1][-LATE:]), levels)
     anywhere = pl.BlockSpec(memory_space=pl.ANY)
     scaled, last, late = pl.pallas_call(
         functools.partial(kernel, sizes, coarse, parts),

time: 101 us -> 101 us (level)
  no operation moved by 1% of the time
where the time goes in v8:
time: 101 us
  Pallas kernels  97.8 us (97%)
  starting transfers between devices  2.05 us (2%)
    pallas_call x1, Pallas kernels, on_device(): pl.pallas_call(functools.partial(kernel, sizes, coarse, parts), out_shape...  93.7 us
    pallas_call x1, Pallas kernels, on_device(): pl.pallas_call(functools.partial(write_out, small[2]), out_shape=(there,...  3.23 us
    ppermute x1, starting transfers between devices, on_device(): lax.ppermute(late, 'rows', [(r, (r + off) % n) for r in range(n)])  2.05 us
  transfers between devices with their start and end apart: 1, of which 0 were waited for; matrix products, arithmetic and copies ran while one was open for 0% of the time, Pallas kernels for 3%

profile of v8, /device:TPU:0, one launch (start us, length us, event | category | flops | bytes accessed | tf_op | source)
XLA Modules:
  0.0 100.5 jit_solution(9559942697872027368)
XLA Ops:
  0.6 93.7 %heat_steps.1 = (f32[16,4,128,128]{3,2,1,0:T(8,128)S(1)}, f32[16,4,128,128]{3,2,1,0:T(8,128)S(1)}, f32[2,2,32,128]{3,2,1,0:T(8,128)S(1)}) custom-call(f32[16,4,128,128]{3,2,1,0:T(8,128)} %field.1, f32[16,4,128,128]{3,2,1,0:T(8,128)} %conductance.1, f32[16,4,128,128]{3,2,1,0:T(8,128)} %source.1), custom_call_target="tpu_custom_call" | custom-call | tf_op jit(solution)/shard_map/heat_steps/pallas_call | solution.py:488
  94.3 2.1 %collective-permute-start = (f32[2,2,32,128]{3,2,1,0:T(8,128)S(1)}, f32[2,2,32,128]{3,2,1,0:T(8,128)S(1)}, u32[]{:S(2)}, u32[]{:S(2)}) collective-permute-start(f32[2,2,32,128]{3,2,1,0:T(8,128)S(1)} %get-tuple-element.10.late), channel_id=1, source_target_pairs={{0,16},{16,0},{1,17},{17,1},{2,18},{18,2},{3,19},{19,3},{4,20},{20... | collective-permute-start | bytes 196616 | tf_op jit(solution)/shard_map/ppermute | solution.py:516
  96.4 3.2 %write_out.1 = (f32[16,4,128,128]{3,2,1,0:T(8,128)}, f32[16,4,128,128]{3,2,1,0:T(8,128)}) custom-call(f32[16,4,128,128]{3,2,1,0:T(8,128)S(1)} %get-tuple-element.7.near_anomaly, f32[16,4,128,128]{3,2,1,0:T(8,128)S(1)} %get-tuple-element.8.near_field), custom_call_target="tpu_custom_call" | custom-call | bytes 16777216 | tf_op jit(solution)/shard_map/write_out/pallas_call | solution.py:520
  99.6 0.0 collective-permute-done.refs_0_
  99.6 0.9 write_late.1
Async XLA Ops:
  94.3 5.3 %collective-permute-start = (f32[2,2,32,128]{3,2,1,0:T(8,128)S(1)}, f32[2,2,32,128]{3,2,1,0:T(8,128)S(1)}, u32[]{:S(2)}, u32[]{:S(2)}) collective-permute-start(f32[2,2,32,128]{3,2,1,0:T(8,128)S(1)} %get-tuple-element.10.late), channel_id=1, source_target_pairs={{0,16},{16,0},{1,17},{17,1},{2,18},{18,2},{3,19},{19,3},{4,20},{20... | collective-permute-start | bytes 196616 | tf_op jit(solution)/shard_map/ppermute | solution.py:516

commit v9 on v8

--- a/solution.py
+++ b/solution.py
@@ -9,7 +9,7 @@
 
 STEPS = 4
 TILE = 8
-PIECES = 4
+PIECES = 2
 FINE = (4, 3)
 LATE = 2
 YIELD = 1

time: 101 us -> 101 us (level)
  no operation moved by 1% of the time
where the time goes in v9:
time: 101 us; the launch traced here: 100 us
  Pallas kernels  97.7 us (97%)
  starting transfers between devices  2.05 us (2%)
    pallas_call x1, Pallas kernels, on_device(): pl.pallas_call(functools.partial(kernel, sizes, coarse, parts), out_shape...  93.7 us
    pallas_call x1, Pallas kernels, on_device(): pl.pallas_call(functools.partial(write_out, small[2]), out_shape=(there,...  3.18 us
    ppermute x1, starting transfers between devices, on_device(): lax.ppermute(late, 'rows', [(r, (r + off) % n) for r in range(n)])  2.05 us
  transfers between devices with their start and end apart: 1, of which 0 were waited for; matrix products, arithmetic and copies ran while one was open for 0% of the time, Pallas kernels for 3%

profile of v9, /device:TPU:0, one launch (start us, length us, event | category | flops | bytes accessed | tf_op | source)
XLA Modules:
  0.0 100.4 jit_solution(492019090987209639)
XLA Ops:
  0.6 93.7 %heat_steps.1 = (f32[16,4,128,128]{3,2,1,0:T(8,128)S(1)}, f32[16,4,128,128]{3,2,1,0:T(8,128)S(1)}, f32[2,2,32,128]{3,2,1,0:T(8,128)S(1)}) custom-call(f32[16,4,128,128]{3,2,1,0:T(8,128)} %field.1, f32[16,4,128,128]{3,2,1,0:T(8,128)} %conductance.1, f32[16,4,128,128]{3,2,1,0:T(8,128)} %source.1), custom_call_target="tpu_custom_call" | custom-call | tf_op jit(solution)/shard_map/heat_steps/pallas_call | solution.py:488
  94.3 2.1 %collective-permute-start = (f32[2,2,32,128]{3,2,1,0:T(8,128)S(1)}, f32[2,2,32,128]{3,2,1,0:T(8,128)S(1)}, u32[]{:S(2)}, u32[]{:S(2)}) collective-permute-start(f32[2,2,32,128]{3,2,1,0:T(8,128)S(1)} %get-tuple-element.10.late), channel_id=1, source_target_pairs={{0,16},{16,0},{1,17},{17,1},{2,18},{18,2},{3,19},{19,3},{4,20},{20... | collective-permute-start | bytes 196616 | tf_op jit(solution)/shard_map/ppermute | solution.py:516
  96.4 3.2 %write_out.1 = (f32[16,4,128,128]{3,2,1,0:T(8,128)}, f32[16,4,128,128]{3,2,1,0:T(8,128)}) custom-call(f32[16,4,128,128]{3,2,1,0:T(8,128)S(1)} %get-tuple-element.7.near_anomaly, f32[16,4,128,128]{3,2,1,0:T(8,128)S(1)} %get-tuple-element.8.near_field), custom_call_target="tpu_custom_call" | custom-call | bytes 16777216 | tf_op jit(solution)/shard_map/write_out/pallas_call | solution.py:520
  99.6 0.0 collective-permute-done.refs_0_
  99.6 0.9 write_late.1
Async XLA Ops:
  94.3 5.2 %collective-permute-start = (f32[2,2,32,128]{3,2,1,0:T(8,128)S(1)}, f32[2,2,32,128]{3,2,1,0:T(8,128)S(1)}, u32[]{:S(2)}, u32[]{:S(2)}) collective-permute-start(f32[2,2,32,128]{3,2,1,0:T(8,128)S(1)} %get-tuple-element.10.late), channel_id=1, source_target_pairs={{0,16},{16,0},{1,17},{17,1},{2,18},{18,2},{3,19},{19,3},{4,20},{20... | collective-permute-start | bytes 196616 | tf_op jit(solution)/shard_map/ppermute | solution.py:516
